TPU v7x, 32 devices: a whole 2x2x4 slice. The times are simulated.
32 devices in a mesh: dp: 4 (over y, x), expert: 8 (over z, core).
Axes of the slice: x: 2, y: 2, z: 4, core: 2. Of those that a mesh axis runs over, the one named last changes fastest.
Arguments:
- tokens: bfloat16 [4096, 2048], P(('dp', 'expert')), may hold values from -6 to 6
- expert_ids: int32 [4096, 2], P(('dp', 'expert')), may hold values from 0 to 7, all different within a row; in each aligned block of 128 rows (0 to 127, 128 to 255, ...) at most 40 rows name the same one
- gate_units: int32 [4096, 2], P(('dp', 'expert')), may hold values from 64 to 1023
- capacity: int32 [8], replicated, may hold values from 512 to 1535
- w_gate: bfloat16 [8, 2048, 1408], P('expert', None, 'dp'), may hold values from -0.125 to 0.125
- w_up: bfloat16 [8, 2048, 1408], P('expert', None, 'dp'), may hold values from -0.125 to 0.125
- w_down: bfloat16 [8, 2048, 1408], P('expert', None, 'dp'), may hold values from -0.15625 to 0.15625
Outputs:
- mixed: bfloat16 [4096, 2048], P(('dp', 'expert'))
Inputs may be any that keep to these rules, and one draw needn't show every extreme that they name: `expert_ids`: each row names two different experts; of one device's 128 rows (aligned blocks) no expert is named more than 40 times.
All inputs are finite; a program needn't handle non-finite values.
Results may differ from a plain program's by a relative error of at most 0.0057.
Values may be sent and summed in bfloat16 or wider, within the bound.
No kernel may reach another device: no remote copies, remote signals or barrier semaphores. Data moves between devices by JAX's collectives and lax.ppermute only.
A program may use at most 128 MiB of HBM per device.

v0:
```python
import jax
import jax.numpy as jnp
from jax import lax
from jax.sharding import PartitionSpec as P


def prefix(shard, axis, combine, identity):
    length, here = (lax.axis_size(axis), lax.axis_index(axis))
    everything = lax.all_gather(shard, axis)
    start = jnp.broadcast_to(jnp.asarray(identity, shard.dtype), shard.shape)

    def step(k, before):
        reached = k < here
        new = combine(before, everything[k])
        return jnp.where(reached, new, before)

    return lax.fori_loop(0, length, step, start)


def expert_rows(rows, gate_w, up_w, down_w):
    gate = jnp.dot(rows, gate_w, preferred_element_type=jnp.float32)
    up = jnp.dot(rows, up_w, preferred_element_type=jnp.float32)
    hidden = (jax.nn.silu(gate) * up).astype(jnp.bfloat16)
    return lax.dot_general(
        hidden, down_w, (((1,), (1,)), ((), ())), preferred_element_type=jnp.float32
    )


def add_counts(earlier, later):
    return earlier + later


def local(tokens, expert_ids, gate_units, capacity, w_gate, w_up, w_down):
    tok_rows = tokens.shape[0]
    width = tokens.shape[1]
    n_experts = capacity.shape[0]
    most = max(2, 5 * tok_rows // (2 * n_experts))
    slots_all = n_experts * most
    flat = expert_ids.reshape(-1)
    onehot = (flat[:, None] == jnp.arange(n_experts, dtype=jnp.int32)[None, :]).astype(jnp.int32)
    local_rank = jnp.sum((jnp.cumsum(onehot, axis=0) - onehot) * onehot, axis=1)
    counts = jnp.sum(onehot, axis=0)
    offsets = prefix(counts, ("dp", "expert"), add_counts, jnp.zeros_like(counts))
    global_slot = jnp.sum(onehot * offsets[None, :], axis=1) + local_rank
    limit = jnp.sum(onehot * capacity[None, :], axis=1)
    kept = global_slot < limit
    weight = jnp.where(kept, gate_units.reshape(-1).astype(jnp.float32) / 1024.0, jnp.float32(0.0))
    send_slot = flat * most + local_rank
    chosen = (send_slot[None, :] == jnp.arange(slots_all, dtype=jnp.int32)[:, None]) & kept[None, :]
    placing = jnp.sum(chosen.reshape(slots_all, tok_rows, 2).astype(jnp.int32), axis=2).astype(
        jnp.bfloat16
    )
    outgoing = jnp.dot(placing, tokens, preferred_element_type=jnp.float32).astype(jnp.bfloat16)
    outgoing = outgoing.reshape(n_experts, most, width)
    arrived = lax.all_to_all(outgoing, "expert", split_axis=0, concat_axis=0, tiled=True).reshape(
        slots_all, width
    )
    produced = expert_rows(
        arrived,
        lax.all_gather(w_gate, "dp", axis=2, tiled=True)[0],
        lax.all_gather(w_up, "dp", axis=2, tiled=True)[0],
        lax.all_gather(w_down, "dp", axis=2, tiled=True)[0],
    )
    answer = produced.astype(jnp.bfloat16).reshape(n_experts, most, width)
    back = lax.all_to_all(answer, "expert", split_axis=0, concat_axis=0, tiled=True).reshape(
        slots_all, width
    )
    picked = back[send_slot].astype(jnp.float32) * weight[:, None]
    mixed = jnp.sum(picked.reshape(tok_rows, 2, width), axis=1)
    return mixed.astype(jnp.bfloat16)


def solution(mesh):
    return jax.shard_map(
        local,
        mesh=mesh,
        in_specs=(
            P(("dp", "expert"), None),
            P(("dp", "expert"), None),
            P(("dp", "expert"), None),
            P(),
            P("expert", None, "dp"),
            P("expert", None, "dp"),
            P("expert", None, "dp"),
        ),
        out_specs=P(("dp", "expert"), None),
        check_vma=False,
    )
```

profile of v0, /device:TPU:0, one launch (start us, length us, event | category | flops | bytes accessed | tf_op | source)
XLA Modules:
  0.0 275.7 jit_solution(2728513415111079550)
XLA Ops:
  6.5 0.0 copy-start
  6.5 0.0 all-gather.5.cloned.1.call-start
  6.5 0.7 all-gather.5.cloned.1.call-update
  7.3 0.0 copy-start.1
  7.3 0.0 copy-start.3
  7.3 0.0 copy-start.2
  7.3 0.0 all-gather.7.cloned.1.call-start
  7.3 0.7 all-gather.7.cloned.1.call-update
  8.0 0.0 all-gather.9.cloned.1.call-start
  8.1 0.7 all-gather.9.cloned.1.call-update
  8.8 0.0 copy-done.1
  8.8 0.1 copy.23
  8.9 0.1 eq.39
  9.1 0.1 eq.43
  9.2 0.1 convert_reduce_fusion.1
  9.3 0.2 dynamic-update-slice
  9.6 42.6 %all-reduce = s32[256]{0:T(256)S(1)} all-reduce(s32[256]{0:T(256)S(1)} %dynamic-update-slice), channel_id=2, replica_groups=mesh['dp'=4,'expert'=8] {'dp','expert'}, use_global_device_ids=true, to_apply=%add | all-reduce | flops 256 | bytes 2048
  52.1 0.1 reshape.134
  52.2 0.6 reduce-window.6
  52.8 0.2 slice_reduce_fusion
  53.1 1.3 while.14
  54.4 0.0 copy-done.3
  54.4 0.1 select_reduce_fusion.1
  54.5 0.1 reduce_sum.63
  54.6 0.1 copy.28
  54.7 0.2 reduce_sum.66
  54.8 0.1 copy.27
  54.9 0.2 reduce_sum.68
  55.1 0.1 copy.29
  55.2 0.1 copy.26
  55.2 0.0 copy-done.2
  55.3 0.0 copy-done
  55.3 0.5 convolution_convert_fusion
  55.8 35.6 %all_to_all.10 = bf16[8,40,2048]{2,1,0:T(8,128)(2,1)S(1)} all-to-all(bf16[8,40,2048]{2,1,0:T(8,128)(2,1)S(1)} %bitcast.35), channel_id=1, replica_groups=mesh['dp'=4,'expert'=8] {'expert'}, dimensions={0} | all-to-all | bytes 2621440 | tf_op jit(solution)/shard_map/all_to_all | solution.py:55
  91.4 0.0 all-gather.5.cloned.1.call-done
  91.4 6.1 %fusion.4 = f32[320,1408]{1,0:T(8,128)} fusion(bf16[320,2048]{1,0:T(8,128)(2,1)S(1)} %bitcast.36, bf16[1,2048,1408]{1,2,0:T(8,128)(2,1)} %all-gather.5.cloned.1.call-done), kind=kOutput, calls=%fused_computation.7 | convolution fusion | flops 1845493760 | bytes 8880128 | tf_op jit(solution)/shard_map/dot_general | solution.py:21
  97.5 48.3 %all-gather.7.cloned.1.call-done = bf16[1,2048,1408]{1,2,0:T(8,128)(2,1)} async-done(((bf16[1,2048,352]{1,2,0:T(8,128)(2,1)}), bf16[1,2048,1408]{1,2,0:T(8,128)(2,1)}) %all-gather.7.cloned.1.call-update) | async-done | bytes 5767184 | tf_op jit(solution)/shard_map/all_gather | solution.py:61
  145.8 67.5 %all-gather.9.cloned.1.call-done = bf16[1,2048,1408]{1,2,0:T(8,128)(2,1)} async-done(((bf16[1,2048,352]{1,2,0:T(8,128)(2,1)}), bf16[1,2048,1408]{1,2,0:T(8,128)(2,1)}) %all-gather.9.cloned.1.call-update) | async-done | bytes 5767184 | tf_op jit(solution)/shard_map/all_gather | solution.py:62
  213.4 10.3 %fusion.9 = bf16[320,2048]{1,0:T(8,128)(2,1)} fusion(bf16[1,2048,1408]{1,2,0:T(8,128)(2,1)} %all-gather.9.cloned.1.call-done, bf16[320,2048]{1,0:T(8,128)(2,1)S(1)} %bitcast.37, bf16[1,2048,1408]{1,2,0:T(8,128)(2,1)} %all-gather.7.cloned.1.call-done, f32[320,1408]{1,0:T(8,128)} %fusion.4), kind=kOutput, calls=%fused_computation.10 | convolution fusion | flops 3694346240 | bytes 15958016 | tf_op jit(solution)/shard_map/dot_general | solution.py:24
  223.7 4.6 %all-to-all-start.1 = ((bf16[8,40,2048]{2,1,0:T(8,128)(2,1)}), bf16[8,40,2048]{2,1,0:T(8,128)(2,1)S(1)}, u32[]{:S(2)}, u32[]{:S(2)}) async-start(bf16[8,40,2048]{2,1,0:T(8,128)(2,1)} %bitcast.7), calls=%async_computation.1 | async-start | bytes 2621440 | tf_op jit(solution)/shard_map/all_to_all | solution.py:65
  228.3 0.1 mul.68
  228.4 0.1 copy.30
  228.5 31.9 %all-to-all-done.1 = bf16[8,40,2048]{2,1,0:T(8,128)(2,1)S(1)} async-done(((bf16[8,40,2048]{2,1,0:T(8,128)(2,1)}), bf16[8,40,2048]{2,1,0:T(8,128)(2,1)S(1)}, u32[]{:S(2)}, u32[]{:S(2)}) %all-to-all-start.1) | async-done | bytes 1310752 | tf_op jit(solution)/shard_map/all_to_all | solution.py:65
  260.5 2.3 gather_fusion
  262.8 2.4 reshape.125
  265.2 4.0 %multiply_reduce_fusion = bf16[128,2048]{1,0:T(8,128)(2,1)} fusion(f32[128,2,2048]{2,1,0:T(2,128)S(1)} %reshape.125, f32[128,2]{1,0:T(8,128)S(1)} %copy.30), kind=kLoop, calls=%fused_computation.13 | loop fusion | flops 786432 | bytes 2622464 | tf_op jit(solution)/shard_map/reduce_sum | solution.py:69
  (42 shorter events, 0.7 us)
Async XLA Ops:
  6.5 48.8 %copy-start = (bf16[128,2048]{1,0:T(8,128)(2,1)S(1)}, bf16[128,2048]{1,0:T(8,128)(2,1)}, u32[]{:S(2)}) copy-start(bf16[128,2048]{1,0:T(8,128)(2,1)} %param.9) | copy-start | bytes 1572868
  6.5 84.9 %all-gather.5.cloned.1.call-start = ((), (), s32[]{:S(2)}) async-start(), calls=%async_computation.2 | async-start | bytes 7208960 | tf_op jit(solution)/shard_map/all_gather | solution.py:60
  7.3 1.5 copy-start.1
  7.3 47.1 %copy-start.3 = (s32[8]{0:T(128)S(1)}, s32[8]{0:T(128)}, u32[]{:S(2)}) copy-start(s32[8]{0:T(128)} %param.12) | copy-start | bytes 100
  7.3 47.9 %copy-start.2 = (s32[128,2]{0,1:T(2,128)S(1)}, s32[128,2]{0,1:T(2,128)}, u32[]{:S(2)}) copy-start(s32[128,2]{0,1:T(2,128)} %param.11) | copy-start | bytes 3076
  7.3 138.6 %all-gather.7.cloned.1.call-start = ((), (), s32[]{:S(2)}) async-start(), calls=%async_computation.3 | async-start | bytes 7208960 | tf_op jit(solution)/shard_map/all_gather | solution.py:61
  8.0 205.4 %all-gather.9.cloned.1.call-start = ((), (), s32[]{:S(2)}) async-start(), calls=%async_computation.4 | async-start | bytes 7208960 | tf_op jit(solution)/shard_map/all_gather | solution.py:62
  223.7 36.8 %all-to-all-start.1 = ((bf16[8,40,2048]{2,1,0:T(8,128)(2,1)}), bf16[8,40,2048]{2,1,0:T(8,128)(2,1)S(1)}, u32[]{:S(2)}, u32[]{:S(2)}) async-start(bf16[8,40,2048]{2,1,0:T(8,128)(2,1)} %bitcast.7), calls=%async_computation.1 | async-start | bytes 2621440 | tf_op jit(solution)/shard_map/all_to_all | solution.py:65
Sparse Core Ops, SparseCore 0:
  9.2 69.0 all-gather.4
  80.1 65.6 all-gather.6
  147.7 65.6 all-gather.8
where the time goes:
time: 276 us
  waiting for transfers between devices  150 us (54%)
  blocking collectives  78.1 us (28%)
  matrix products  16.9 us (6%)
  between operations  13.3 us (5%)
  local copies, waits for them, and re-layouts  6.6 us (2%)
  other arithmetic  5.55 us (2%)
  starting transfers between devices  4.68 us (2%)
    all_gather x1, waiting for transfers between devices, local(): lax.all_gather(w_down, 'dp', axis=2, tiled=True)[0]  67.5 us
    all_gather x1, waiting for transfers between devices, local(): lax.all_gather(w_up, 'dp', axis=2, tiled=True)[0]  48.3 us
    unnamed x1, blocking collectives  42.6 us
    all_to_all x1, blocking collectives, local(): lax.all_to_all(outgoing, 'expert', split_axis=0, concat_axis=0, tiled=True)  35.6 us
    all_to_all x1, waiting for transfers between devices, local(): lax.all_to_all(answer, 'expert', split_axis=0, concat_axis=0, tiled=True)  31.9 us
    dot_general x1, matrix products, expert_rows(): lax.dot_general(hidden, down_w, (((1,), (1,)), ((), ())), preferred_eleme...  10.3 us
    dot_general x1, matrix products, expert_rows(): gate = jnp.dot(rows, gate_w, preferred_element_type=jnp.float32)  6.11 us
  transfers between devices with their start and end apart: 4, of which 3 were waited for; matrix products, arithmetic and copies ran while one was open for 4% of the time, Pallas kernels for 0%

commit v1 on v0

--- a/solution.py
+++ b/solution.py
@@ -1,7 +1,15 @@
+import functools
 import jax
 import jax.numpy as jnp
 from jax import lax
 from jax.sharding import PartitionSpec as P
+
+
+def render_screen_for(panel, out_dim):
+    return jnp.concatenate(jax.lax.all_gather(panel, "dp"), axis=out_dim)
+
+
+joints_begin = functools.partial(render_screen_for, out_dim=2)
 
 
 def prefix(shard, axis, combine, identity):
@@ -59,7 +67,7 @@
         arrived,
         lax.all_gather(w_gate, "dp", axis=2, tiled=True)[0],
         lax.all_gather(w_up, "dp", axis=2, tiled=True)[0],
-        lax.all_gather(w_down, "dp", axis=2, tiled=True)[0],
+        joints_begin(w_down)[0],
     )
     answer = produced.astype(jnp.bfloat16).reshape(n_experts, most, width)
     back = lax.all_to_all(answer, "expert", split_axis=0, concat_axis=0, tiled=True).reshape(

time: 276 us -> 276 us (level)
  no operation moved by 1% of the time
where the time goes in v1:
time: 276 us
  waiting for transfers between devices  150 us (54%)
  blocking collectives  78.1 us (28%)
  matrix products  16.9 us (6%)
  between operations  13.3 us (5%)
  local copies, waits for them, and re-layouts  6.6 us (2%)
  other arithmetic  5.55 us (2%)
  starting transfers between devices  4.68 us (2%)
    all_gather x1, waiting for transfers between devices, render_screen_for(): return jnp.concatenate(jax.lax.all_gather(panel, 'dp'), axis=out_dim)  67.5 us
    all_gather x1, waiting for transfers between devices, local(): lax.all_gather(w_up, 'dp', axis=2, tiled=True)[0]  48.3 us
    unnamed x1, blocking collectives  42.6 us
    all_to_all x1, blocking collectives, local(): lax.all_to_all(outgoing, 'expert', split_axis=0, concat_axis=0, tiled=True)  35.6 us
    all_to_all x1, waiting for transfers between devices, local(): lax.all_to_all(answer, 'expert', split_axis=0, concat_axis=0, tiled=True)  31.9 us
    dot_general x1, matrix products, expert_rows(): lax.dot_general(hidden, down_w, (((1,), (1,)), ((), ())), preferred_eleme...  10.3 us
    dot_general x1, matrix products, expert_rows(): gate = jnp.dot(rows, gate_w, preferred_element_type=jnp.float32)  6.11 us
  transfers between devices with their start and end apart: 4, of which 3 were waited for; matrix products, arithmetic and copies ran while one was open for 4% of the time, Pallas kernels for 0%

profile of v1, /device:TPU:0, one launch (start us, length us, event | category | flops | bytes accessed | tf_op | source)
XLA Modules:
  0.0 275.7 jit_solution(5200091513108538925)
XLA Ops:
  6.5 0.0 copy-start
  6.5 0.0 all-gather.6.cloned.1.call-start
  6.5 0.7 all-gather.6.cloned.1.call-update
  7.3 0.0 copy-start.1
  7.3 0.0 copy-start.3
  7.3 0.0 copy-start.2
  7.3 0.0 all-gather.8.cloned.1.call-start
  7.3 0.7 all-gather.8.cloned.1.call-update
  8.0 0.0 all-gather.10.cloned.1.call-start
  8.1 0.7 all-gather.10.cloned.1.call-update
  8.8 0.0 copy-done.1
  8.8 0.1 copy.28
  8.9 0.1 eq.39
  9.1 0.1 eq.43
  9.2 0.1 convert_reduce_fusion.1
  9.3 0.2 dynamic-update-slice
  9.6 42.6 %all-reduce = s32[256]{0:T(256)S(1)} all-reduce(s32[256]{0:T(256)S(1)} %dynamic-update-slice), channel_id=2, replica_groups=mesh['dp'=4,'expert'=8] {'dp','expert'}, use_global_device_ids=true, to_apply=%add | all-reduce | flops 256 | bytes 2048
  52.1 0.1 reshape.138
  52.2 0.6 reduce-window.6
  52.8 0.2 slice_reduce_fusion
  53.1 1.3 while.14
  54.4 0.0 copy-done.3
  54.4 0.1 select_reduce_fusion.1
  54.5 0.1 reduce_sum.63
  54.6 0.1 copy.33
  54.7 0.2 reduce_sum.66
  54.8 0.1 copy.32
  54.9 0.2 reduce_sum.68
  55.1 0.1 copy.34
  55.2 0.1 copy.31
  55.2 0.0 copy-done.2
  55.3 0.0 copy-done
  55.3 0.5 convolution_convert_fusion.1
  55.8 35.6 %all_to_all.10 = bf16[8,40,2048]{2,1,0:T(8,128)(2,1)S(1)} all-to-all(bf16[8,40,2048]{2,1,0:T(8,128)(2,1)S(1)} %bitcast.36), channel_id=1, replica_groups=mesh['dp'=4,'expert'=8] {'expert'}, dimensions={0} | all-to-all | bytes 2621440 | tf_op jit(solution)/shard_map/all_to_all | solution.py:63
  91.4 0.0 all-gather.6.cloned.1.call-done
  91.4 6.1 %fusion.2 = f32[320,1408]{1,0:T(8,128)} fusion(bf16[320,2048]{1,0:T(8,128)(2,1)S(1)} %bitcast.37, bf16[1,2048,1408]{1,2,0:T(8,128)(2,1)} %all-gather.6.cloned.1.call-done), kind=kOutput, calls=%fused_computation.5 | convolution fusion | flops 1845493760 | bytes 8880128 | tf_op jit(solution)/shard_map/dot_general | solution.py:29
  97.5 48.3 %all-gather.8.cloned.1.call-done = bf16[1,2048,1408]{1,2,0:T(8,128)(2,1)} async-done(((bf16[1,2048,352]{1,2,0:T(8,128)(2,1)}), bf16[1,2048,1408]{1,2,0:T(8,128)(2,1)}) %all-gather.8.cloned.1.call-update) | async-done | bytes 5767184 | tf_op jit(solution)/shard_map/all_gather | solution.py:69
  145.8 67.5 %all-gather.10.cloned.1.call-done = bf16[4,2048,352]{1,2,0:T(8,128)(2,1)} async-done(((bf16[1,2048,352]{1,2,0:T(8,128)(2,1)}), bf16[4,2048,352]{1,2,0:T(8,128)(2,1)}) %all-gather.10.cloned.1.call-update) | async-done | bytes 5767184 | tf_op jit(solution)/shard_map/all_gather | solution.py:9
  213.4 10.3 %convolution_convert_fusion = bf16[320,2048]{1,0:T(8,128)(2,1)} fusion(bf16[2048,1408]{0,1:T(8,128)(2,1)} %bitcast.41, bf16[320,2048]{1,0:T(8,128)(2,1)S(1)} %bitcast.38, bf16[1,2048,1408]{1,2,0:T(8,128)(2,1)} %all-gather.8.cloned.1.call-done, f32[320,1408]{1,0:T(8,128)} %fusion.2), kind=kOutput, calls=%fused_computation.8 | convolution fusion | flops 3694346240 | bytes 15958016 | tf_op jit(solution)/shard_map/dot_general | solution.py:32
  223.7 4.6 %all-to-all-start.1 = ((bf16[8,40,2048]{2,1,0:T(8,128)(2,1)}), bf16[8,40,2048]{2,1,0:T(8,128)(2,1)S(1)}, u32[]{:S(2)}, u32[]{:S(2)}) async-start(bf16[8,40,2048]{2,1,0:T(8,128)(2,1)} %bitcast.9), calls=%async_computation.1 | async-start | bytes 2621440 | tf_op jit(solution)/shard_map/all_to_all | solution.py:73
  228.3 0.1 mul.68
  228.4 0.1 copy.35
  228.5 31.9 %all-to-all-done.1 = bf16[8,40,2048]{2,1,0:T(8,128)(2,1)S(1)} async-done(((bf16[8,40,2048]{2,1,0:T(8,128)(2,1)}), bf16[8,40,2048]{2,1,0:T(8,128)(2,1)S(1)}, u32[]{:S(2)}, u32[]{:S(2)}) %all-to-all-start.1) | async-done | bytes 1310752 | tf_op jit(solution)/shard_map/all_to_all | solution.py:73
  260.5 2.3 gather_fusion
  262.8 2.4 reshape.129
  265.2 4.0 %multiply_reduce_fusion = bf16[128,2048]{1,0:T(8,128)(2,1)} fusion(f32[128,2,2048]{2,1,0:T(2,128)S(1)} %reshape.129, f32[128,2]{1,0:T(8,128)S(1)} %copy.35), kind=kLoop, calls=%fused_computation.11 | loop fusion | flops 786432 | bytes 2622464 | tf_op jit(solution)/shard_map/reduce_sum | solution.py:77
  (42 shorter events, 0.7 us)
Async XLA Ops:
  6.5 48.8 %copy-start = (bf16[128,2048]{1,0:T(8,128)(2,1)S(1)}, bf16[128,2048]{1,0:T(8,128)(2,1)}, u32[]{:S(2)}) copy-start(bf16[128,2048]{1,0:T(8,128)(2,1)} %param.9) | copy-start | bytes 1572868
  6.5 84.9 %all-gather.6.cloned.1.call-start = ((), (), s32[]{:S(2)}) async-start(), calls=%async_computation.2 | async-start | bytes 7208960 | tf_op jit(solution)/shard_map/all_gather | solution.py:68
  7.3 1.5 copy-start.1
  7.3 47.1 %copy-start.3 = (s32[8]{0:T(128)S(1)}, s32[8]{0:T(128)}, u32[]{:S(2)}) copy-start(s32[8]{0:T(128)} %param.12) | copy-start | bytes 100
  7.3 47.9 %copy-start.2 = (s32[128,2]{0,1:T(2,128)S(1)}, s32[128,2]{0,1:T(2,128)}, u32[]{:S(2)}) copy-start(s32[128,2]{0,1:T(2,128)} %param.11) | copy-start | bytes 3076
  7.3 138.6 %all-gather.8.cloned.1.call-start = ((), (), s32[]{:S(2)}) async-start(), calls=%async_computation.3 | async-start | bytes 7208960 | tf_op jit(solution)/shard_map/all_gather | solution.py:69
  8.0 205.4 %all-gather.10.cloned.1.call-start = ((), (), s32[]{:S(2)}) async-start(), calls=%async_computation.4 | async-start | bytes 7208960 | tf_op jit(solution)/shard_map/all_gather | solution.py:9
  223.7 36.8 %all-to-all-start.1 = ((bf16[8,40,2048]{2,1,0:T(8,128)(2,1)}), bf16[8,40,2048]{2,1,0:T(8,128)(2,1)S(1)}, u32[]{:S(2)}, u32[]{:S(2)}) async-start(bf16[8,40,2048]{2,1,0:T(8,128)(2,1)} %bitcast.9), calls=%async_computation.1 | async-start | bytes 2621440 | tf_op jit(solution)/shard_map/all_to_all | solution.py:73
Sparse Core Ops, SparseCore 0:
  9.2 69.0 all-gather.5
  80.1 65.6 all-gather.7
  147.7 65.6 all-gather.9
